TPU v7x, 32 devices: a whole 2x2x4 slice. The times are simulated.
32 devices in a mesh: segment: 8 (over z, x), dp: 4 (over y, core).
Axes of the slice: x: 2, y: 2, z: 4, core: 2. Of those that a mesh axis runs over, the one named last changes fastest.
Arguments:
- src_embed: bfloat16 [16, 128, 2048], P('dp', None, 'segment'), parts along dimension 0, may hold values from -6 to 6
- tgt_embed: bfloat16 [16, 128, 2048], P('dp', None, 'segment'), parts along dimension 0, may hold values from -6 to 6
- src_lengths: int32 [16], P('dp'), parts along dimension 0, may hold values from 32 to 128
- tgt_lengths: int32 [16], P('dp'), parts along dimension 0, may hold values from 32 to 128
- attn_in: bfloat16 [8, 2048, 3072], P('segment'), may hold values from -0.125 to 0.125
- attn_out: bfloat16 [8, 1024, 2048], P('segment'), may hold values from -0.375 to 0.375
- norm_gain: float32 [4, 2048], replicated, may hold values from 0.25 to 1.75
- final_gain: float32 [2048], replicated, may hold values from 0.25 to 1.75
Outputs:
- decoded: bfloat16 [16, 128, 2048], P('dp', None, 'segment'), parts along dimension 0
There are 4 independent parts, one for each index of `dp`. A program takes and returns all parts, laid end to end along the dimension named above; an argument that names none is the same for every part. Nothing has to cross between parts.
Inputs may be any that keep to these rules, and one draw needn't show every extreme that they name: `src_lengths`: keys at positions below a sequence's length are its real tokens. `tgt_lengths`: keys at positions below a sequence's length are its real tokens.
All inputs are finite; a program needn't handle non-finite values.
Results may differ from a plain program's by a relative error of at most 0.015.
Values may be sent and summed in bfloat16 or wider, within the bound.
A program may use at most 64 MiB of HBM per device.

v0:
```python
import jax
import jax.numpy as jnp
from jax import lax
from jax.sharding import PartitionSpec as P

HEAD = 64
epsilon = 1e-06
score_scale = 0.125


def partner(value, axis, distance):
    mask = 2**distance
    pairs = [(source, source ^ mask) for source in range(lax.axis_size(axis))]
    return lax.ppermute(value, axis, pairs)


def shifted(value, axis, by):
    length = lax.axis_size(axis)
    pairs = [(i, i + by) for i in range(length) if 0 <= i + by < length]
    return lax.ppermute(value, axis, pairs)


def rms_scale(values, gain_vector):
    return (
        values
        * lax.rsqrt(jnp.mean(values * values, axis=-1, keepdims=True) + epsilon)
        * gain_vector
    )


def attention(queries, key_rows, values, allowed):
    head_count = queries.shape[1] // HEAD
    shaped_q = queries.reshape(queries.shape[0], head_count, HEAD)
    shaped_k = key_rows.reshape(key_rows.shape[0], head_count, HEAD)
    shaped_v = values.reshape(values.shape[0], head_count, HEAD)
    scores = (
        jnp.einsum("qhd,khd->hqk", shaped_q, shaped_k, preferred_element_type=jnp.float32)
        * score_scale
    )
    scores = jnp.where(allowed[None], scores, -1000000000.0)
    weights = jax.nn.softmax(scores, axis=-1).astype(jnp.bfloat16)
    mixture = jnp.einsum("hqk,khd->qhd", weights, shaped_v, preferred_element_type=jnp.float32)
    return mixture.reshape(queries.shape[0], -1).astype(jnp.bfloat16)


def pick_row(array, row_slot):
    return lax.dynamic_index_in_dim(array, row_slot, 0, keepdims=False)


def place_row(array, row_slot, update, keep_flag):
    former = pick_row(array, row_slot)
    return lax.dynamic_update_index_in_dim(array, jnp.where(keep_flag, update, former), row_slot, 0)


def on_device(
    src_embed, tgt_embed, src_lengths, tgt_lengths, attn_in, attn_out, norm_gain, final_gain
):
    segments = lax.axis_size("segment")
    group_size = segments // 4
    bit_count = group_size.bit_length() - 1
    segment_index = lax.axis_index("segment")
    section = segment_index // group_size
    member = segment_index % group_size
    batches, seq_len, column_share = src_embed.shape
    full_width = column_share * segments
    destination = (jnp.arange(segments, dtype=jnp.int32) // group_size)[None, None, :, None]
    outgoing = jnp.where(
        destination == 0,
        src_embed[:, :, None, :],
        jnp.where(destination == 2, tgt_embed[:, :, None, :], jnp.zeros((), jnp.bfloat16)),
    )
    arrived = lax.all_to_all(outgoing, "segment", split_axis=2, concat_axis=2, tiled=True)
    embedded = arrived.reshape(batches, seq_len, full_width)
    in_weight = attn_in[0]
    out_weight = attn_out[0]
    head_cols = out_weight.shape[0]
    layer_gain = pick_row(norm_gain, section)
    positions = jnp.arange(seq_len, dtype=jnp.int32)
    causal = positions[None, :] <= positions[:, None]
    is_target = section == 3
    starts_chain = (section == 0) | (section == 2)

    def allowed_for(batch_slot):
        seq_length = jnp.where(
            is_target, pick_row(tgt_lengths, batch_slot), pick_row(src_lengths, batch_slot)
        )
        return (positions[None, :] < seq_length) & (causal | jnp.logical_not(is_target))

    def head_partial(current, memory, batch_slot):
        normed = rms_scale(current.astype(jnp.float32), layer_gain).astype(jnp.bfloat16)
        source = jnp.where(section == 2, memory, normed)
        queries = jnp.dot(
            normed, in_weight[:, :head_cols], preferred_element_type=jnp.float32
        ).astype(jnp.bfloat16)
        key_value = jnp.dot(
            source, in_weight[:, head_cols:], preferred_element_type=jnp.float32
        ).astype(jnp.bfloat16)
        mixture = attention(
            queries, key_value[:, :head_cols], key_value[:, head_cols:], allowed_for(batch_slot)
        )
        return jnp.dot(mixture, out_weight, preferred_element_type=jnp.float32)

    def combine_heads(current, partial_sum):
        summed = partial_sum
        for bit_index in range(bit_count):
            summed = summed + partner(summed, "segment", bit_index)
        return (current.astype(jnp.float32) + summed).astype(jnp.bfloat16)

    def final_norm(output):
        return rms_scale(output.astype(jnp.float32), final_gain).astype(jnp.bfloat16)

    zero_sum = jnp.zeros((seq_len, full_width), jnp.float32)

    def run_sublayer(step_index, received):
        slot_raw = step_index - section
        active = (slot_raw >= 0) & (slot_raw < batches)
        batch_slot = jnp.clip(slot_raw, 0, batches - 1)
        current = jnp.where(starts_chain, pick_row(embedded, batch_slot), received)
        partial_sum = lax.cond(
            active,
            lambda value_in, memory_in: head_partial(value_in, memory_in, batch_slot),
            lambda value_in, memory_in: zero_sum,
            current,
            received,
        )
        output = combine_heads(current, partial_sum)
        return (output, batch_slot, active)

    empty_rows = jnp.zeros((seq_len, full_width), jnp.bfloat16)
    collected = jnp.zeros((batches, seq_len, full_width), jnp.bfloat16)

    def relay_step(step_index, state_tuple):
        received, outputs = state_tuple
        output, batch_slot, active = run_sublayer(step_index, received)
        outputs = place_row(outputs, batch_slot, output, active & (section == 3))
        leaving = jnp.where(section == 1, final_norm(output), output)
        forwarded = shifted(leaving, "segment", group_size)
        return (forwarded, outputs)

    state_tuple = lax.fori_loop(0, batches + 3, relay_step, (empty_rows, collected))
    outputs = state_tuple[1]
    decoded_cols = lax.dynamic_slice_in_dim(outputs, segment_index * column_share, column_share, 2)
    for distance in range(1, 4):
        chosen = lax.dynamic_slice_in_dim(
            outputs, ((3 - distance) * group_size + member) * column_share, column_share, 2
        )
        incoming = shifted(chosen, "segment", -distance * group_size)
        decoded_cols = jnp.where(section == 3 - distance, incoming, decoded_cols)
    return decoded_cols


def solution(mesh):
    in_specs = (
        P("dp", None, "segment"),
        P("dp", None, "segment"),
        P("dp"),
        P("dp"),
        P("segment", None, None),
        P("segment", None, None),
        P(),
        P(),
    )
    out_specs = P("dp", None, "segment")
    return jax.shard_map(
        on_device, mesh=mesh, in_specs=in_specs, out_specs=out_specs, check_vma=False
    )
```

profile of v0, /device:TPU:12, one launch (start us, length us, event | category | flops | bytes accessed | tf_op | source)
XLA Modules:
  0.0 422.6 jit_solution(14281037983660344813)
XLA Ops:
  0.0 2.7 select_select_fusion
  2.7 6.3 %all-to-all-start = ((bf16[4,128,8,256]{3,1,0,2:T(8,128)(2,1)}), bf16[4,128,8,256]{3,1,0,2:T(8,128)(2,1)S(1)}, u32[]{:S(2)}, u32[]{:S(2)}) async-start(bf16[4,128,8,256]{3,1,0,2:T(8,128)(2,1)} %select_select_fusion), calls=%async_computation | async-start | bytes 4194304 | tf_op jit(solution)/shard_map/all_to_all | solution.py:72
  8.9 45.8 %all-to-all-done = bf16[4,128,8,256]{3,1,0,2:T(8,128)(2,1)S(1)} async-done(((bf16[4,128,8,256]{3,1,0,2:T(8,128)(2,1)}), bf16[4,128,8,256]{3,1,0,2:T(8,128)(2,1)S(1)}, u32[]{:S(2)}, u32[]{:S(2)}) %all-to-all-start) | async-done | bytes 2097184 | tf_op jit(solution)/shard_map/all_to_all | solution.py:72
  54.7 2.4 copy.25
  57.1 1.6 broadcast_in_dim.85
  58.7 329.9 %while.18 = (s32[]{:T(128)}, bf16[128,2048]{1,0:T(8,128)(2,1)S(1)}, bf16[4,128,2048]{2,1,0:T(8,128)(2,1)}, pred[]{:T(512)}, pred[]{:T(512)}, /*index=5*/s32[]{:T...) while((s32[]{:T(128)}, bf16[128,2048]{1,0:T(8,128)(2,1)S(1)}, ...), condition=%wide.region_7.8_spmd.clone, body=%wide.region_0.7_spmd.clone.sunk | while | flops 2257898240 | bytes 44399368 | solution.py:140
  58.7 1.1 constant_dynamic-slice_fusion.9
  62.1 23.4 %collective-permute-done = f32[128,2048]{1,0:T(8,128)S(1)} collective-permute-done((f32[128,2048]{1,0:T(8,128)S(1)}, f32[128,2048]{1,0:T(8,128)S(1)}, u32[]{:S(2)}, u32[]{:S(2)}) %collective-permute-start) | collective-permute-done | bytes 1048608 | tf_op jit(solution)/shard_map/while/body/eval_jaxpr/ppermute | solution.py:14
  85.4 1.1 bitcast_dynamic-update-slice_fusion.2
  87.0 1.9 collective-permute-start.1
  88.9 25.8 %collective-permute-done.1 = bf16[128,2048]{1,0:T(8,128)(2,1)S(1)} collective-permute-done((bf16[128,2048]{1,0:T(8,128)(2,1)S(1)}, bf16[128,2048]{1,0:T(8,128)(2,1)S(1)}, u32[]{:S(2)}, u32[]{:S(2)}) %collective-permute-start.1) | collective-permute-done | bytes 524320 | tf_op jit(solution)/shard_map/while/body/eval_jaxpr/ppermute | solution.py:20
  114.7 1.1 constant_dynamic-slice_fusion.9
  116.1 15.2 %conditional.3 = (f32[128,2048]{1,0:T(8,128)S(1)}) conditional(s32[]{:T(128)} %convert_element_type.120, () %tuple.56, (s32[]{:T(128)}, bf16[128,2048]{1,0:T(8,128)(2,1)S(1)}, f32[2048]{0:T(1024)S(1)}, bf16[128,2048]{1,0:T(8,128)(2,1)S(1)}, bf16[2048,3072]{1,0:T(8,128)(2,1)}, /*index=5*/s32[]{:T(128)}, s32[4]{0:T(128)S(1)}, s32[4]{0:T(128)S(1)}, ...), branch_computations={%region_1.1_spmd, %region_2.5_spmd} | conditional | flops 2254227968 | bytes 27479392 | solution.py:119
  118.9 4.7 %fusion.9 = bf16[128,2048]{1,0:T(8,128)(2,1)S(1)} fusion(bf16[2048,3072]{1,0:T(8,128)(2,1)} %get-tuple-element.369, bf16[128,2048]{1,0:T(8,128)(2,1)S(1)} %get-tuple-element.366, pred[]{:T(512)S(6)} %eq.42, bf16[128,2048]{1,0:T(8,128)(2,1)S(1)} %get-tuple-element.367, f32[2048]{0:T(1024)S(1)} %get-tuple-element.368, f32[128]{0:T(128)S(1)} %add_rsqrt_fusion), kind=kOutput, calls=%fused_computation.7 | convolution fusion | flops 1075314688 | bytes 9970177 | tf_op jit(solution)/shard_map/while/body/eval_jaxpr/cond/branch_1_fun/dot_general | solution.py:95
  123.9 2.9 fusion.15
  128.4 2.9 fusion.35
  131.4 2.1 collective-permute-start
  134.5 19.9 %collective-permute-done = f32[128,2048]{1,0:T(8,128)S(1)} collective-permute-done((f32[128,2048]{1,0:T(8,128)S(1)}, f32[128,2048]{1,0:T(8,128)S(1)}, u32[]{:S(2)}, u32[]{:S(2)}) %collective-permute-start) | collective-permute-done | bytes 1048608 | tf_op jit(solution)/shard_map/while/body/eval_jaxpr/ppermute | solution.py:14
  154.5 1.1 bitcast_dynamic-update-slice_fusion.2
  156.0 1.9 collective-permute-start.1
  158.0 10.9 %collective-permute-done.1 = bf16[128,2048]{1,0:T(8,128)(2,1)S(1)} collective-permute-done((bf16[128,2048]{1,0:T(8,128)(2,1)S(1)}, bf16[128,2048]{1,0:T(8,128)(2,1)S(1)}, u32[]{:S(2)}, u32[]{:S(2)}) %collective-permute-start.1) | collective-permute-done | bytes 524320 | tf_op jit(solution)/shard_map/while/body/eval_jaxpr/ppermute | solution.py:20
  168.8 1.1 constant_dynamic-slice_fusion.9
  170.3 15.2 %conditional.3 = (f32[128,2048]{1,0:T(8,128)S(1)}) conditional(s32[]{:T(128)} %convert_element_type.120, () %tuple.56, (s32[]{:T(128)}, bf16[128,2048]{1,0:T(8,128)(2,1)S(1)}, f32[2048]{0:T(1024)S(1)}, bf16[128,2048]{1,0:T(8,128)(2,1)S(1)}, bf16[2048,3072]{1,0:T(8,128)(2,1)}, /*index=5*/s32[]{:T(128)}, s32[4]{0:T(128)S(1)}, s32[4]{0:T(128)S(1)}, ...), branch_computations={%region_1.1_spmd, %region_2.5_spmd} | conditional | flops 2254227968 | bytes 27479392 | solution.py:119
  173.0 4.7 %fusion.9 = bf16[128,2048]{1,0:T(8,128)(2,1)S(1)} fusion(bf16[2048,3072]{1,0:T(8,128)(2,1)} %get-tuple-element.369, bf16[128,2048]{1,0:T(8,128)(2,1)S(1)} %get-tuple-element.366, pred[]{:T(512)S(6)} %eq.42, bf16[128,2048]{1,0:T(8,128)(2,1)S(1)} %get-tuple-element.367, f32[2048]{0:T(1024)S(1)} %get-tuple-element.368, f32[128]{0:T(128)S(1)} %add_rsqrt_fusion), kind=kOutput, calls=%fused_computation.7 | convolution fusion | flops 1075314688 | bytes 9970177 | tf_op jit(solution)/shard_map/while/body/eval_jaxpr/cond/branch_1_fun/dot_general | solution.py:95
  178.0 3.0 fusion.15
  182.6 2.9 fusion.35
  185.5 1.5 collective-permute-start
  188.1 18.7 %collective-permute-done = f32[128,2048]{1,0:T(8,128)S(1)} collective-permute-done((f32[128,2048]{1,0:T(8,128)S(1)}, f32[128,2048]{1,0:T(8,128)S(1)}, u32[]{:S(2)}, u32[]{:S(2)}) %collective-permute-start) | collective-permute-done | bytes 1048608 | tf_op jit(solution)/shard_map/while/body/eval_jaxpr/ppermute | solution.py:14
  206.9 1.1 bitcast_dynamic-update-slice_fusion.2
  208.4 2.5 collective-permute-start.1
  210.9 8.6 %collective-permute-done.1 = bf16[128,2048]{1,0:T(8,128)(2,1)S(1)} collective-permute-done((bf16[128,2048]{1,0:T(8,128)(2,1)S(1)}, bf16[128,2048]{1,0:T(8,128)(2,1)S(1)}, u32[]{:S(2)}, u32[]{:S(2)}) %collective-permute-start.1) | collective-permute-done | bytes 524320 | tf_op jit(solution)/shard_map/while/body/eval_jaxpr/ppermute | solution.py:20
  219.5 1.1 constant_dynamic-slice_fusion.9
  221.0 15.2 %conditional.3 = (f32[128,2048]{1,0:T(8,128)S(1)}) conditional(s32[]{:T(128)} %convert_element_type.120, () %tuple.56, (s32[]{:T(128)}, bf16[128,2048]{1,0:T(8,128)(2,1)S(1)}, f32[2048]{0:T(1024)S(1)}, bf16[128,2048]{1,0:T(8,128)(2,1)S(1)}, bf16[2048,3072]{1,0:T(8,128)(2,1)}, /*index=5*/s32[]{:T(128)}, s32[4]{0:T(128)S(1)}, s32[4]{0:T(128)S(1)}, ...), branch_computations={%region_1.1_spmd, %region_2.5_spmd} | conditional | flops 2254227968 | bytes 27479392 | solution.py:119
  223.7 4.7 %fusion.9 = bf16[128,2048]{1,0:T(8,128)(2,1)S(1)} fusion(bf16[2048,3072]{1,0:T(8,128)(2,1)} %get-tuple-element.369, bf16[128,2048]{1,0:T(8,128)(2,1)S(1)} %get-tuple-element.366, pred[]{:T(512)S(6)} %eq.42, bf16[128,2048]{1,0:T(8,128)(2,1)S(1)} %get-tuple-element.367, f32[2048]{0:T(1024)S(1)} %get-tuple-element.368, f32[128]{0:T(128)S(1)} %add_rsqrt_fusion), kind=kOutput, calls=%fused_computation.7 | convolution fusion | flops 1075314688 | bytes 9970177 | tf_op jit(solution)/shard_map/while/body/eval_jaxpr/cond/branch_1_fun/dot_general | solution.py:95
  228.7 3.0 fusion.15
  233.2 2.9 fusion.35
  236.2 1.2 collective-permute-start
  238.5 17.3 %collective-permute-done = f32[128,2048]{1,0:T(8,128)S(1)} collective-permute-done((f32[128,2048]{1,0:T(8,128)S(1)}, f32[128,2048]{1,0:T(8,128)S(1)}, u32[]{:S(2)}, u32[]{:S(2)}) %collective-permute-start) | collective-permute-done | bytes 1048608 | tf_op jit(solution)/shard_map/while/body/eval_jaxpr/ppermute | solution.py:14
  255.8 1.1 bitcast_dynamic-update-slice_fusion.2
  257.4 3.1 collective-permute-start.1
  260.5 8.0 %collective-permute-done.1 = bf16[128,2048]{1,0:T(8,128)(2,1)S(1)} collective-permute-done((bf16[128,2048]{1,0:T(8,128)(2,1)S(1)}, bf16[128,2048]{1,0:T(8,128)(2,1)S(1)}, u32[]{:S(2)}, u32[]{:S(2)}) %collective-permute-start.1) | collective-permute-done | bytes 524320 | tf_op jit(solution)/shard_map/while/body/eval_jaxpr/ppermute | solution.py:20
  268.5 1.1 constant_dynamic-slice_fusion.9
  269.9 15.2 %conditional.3 = (f32[128,2048]{1,0:T(8,128)S(1)}) conditional(s32[]{:T(128)} %convert_element_type.120, () %tuple.56, (s32[]{:T(128)}, bf16[128,2048]{1,0:T(8,128)(2,1)S(1)}, f32[2048]{0:T(1024)S(1)}, bf16[128,2048]{1,0:T(8,128)(2,1)S(1)}, bf16[2048,3072]{1,0:T(8,128)(2,1)}, /*index=5*/s32[]{:T(128)}, s32[4]{0:T(128)S(1)}, s32[4]{0:T(128)S(1)}, ...), branch_computations={%region_1.1_spmd, %region_2.5_spmd} | conditional | flops 2254227968 | bytes 27479392 | solution.py:119
  272.7 4.7 %fusion.9 = bf16[128,2048]{1,0:T(8,128)(2,1)S(1)} fusion(bf16[2048,3072]{1,0:T(8,128)(2,1)} %get-tuple-element.369, bf16[128,2048]{1,0:T(8,128)(2,1)S(1)} %get-tuple-element.366, pred[]{:T(512)S(6)} %eq.42, bf16[128,2048]{1,0:T(8,128)(2,1)S(1)} %get-tuple-element.367, f32[2048]{0:T(1024)S(1)} %get-tuple-element.368, f32[128]{0:T(128)S(1)} %add_rsqrt_fusion), kind=kOutput, calls=%fused_computation.7 | convolution fusion | flops 1075314688 | bytes 9970177 | tf_op jit(solution)/shard_map/while/body/eval_jaxpr/cond/branch_1_fun/dot_general | solution.py:95
  277.6 2.9 fusion.15
  282.2 2.9 fusion.35
  286.9 15.9 %collective-permute-done = f32[128,2048]{1,0:T(8,128)S(1)} collective-permute-done((f32[128,2048]{1,0:T(8,128)S(1)}, f32[128,2048]{1,0:T(8,128)S(1)}, u32[]{:S(2)}, u32[]{:S(2)}) %collective-permute-start) | collective-permute-done | bytes 1048608 | tf_op jit(solution)/shard_map/while/body/eval_jaxpr/ppermute | solution.py:14
  302.7 1.1 bitcast_dynamic-update-slice_fusion.2
  304.3 3.4 collective-permute-start.1
  307.7 7.7 %collective-permute-done.1 = bf16[128,2048]{1,0:T(8,128)(2,1)S(1)} collective-permute-done((bf16[128,2048]{1,0:T(8,128)(2,1)S(1)}, bf16[128,2048]{1,0:T(8,128)(2,1)S(1)}, u32[]{:S(2)}, u32[]{:S(2)}) %collective-permute-start.1) | collective-permute-done | bytes 524320 | tf_op jit(solution)/shard_map/while/body/eval_jaxpr/ppermute | solution.py:20
  318.4 14.2 %collective-permute-done = f32[128,2048]{1,0:T(8,128)S(1)} collective-permute-done((f32[128,2048]{1,0:T(8,128)S(1)}, f32[128,2048]{1,0:T(8,128)S(1)}, u32[]{:S(2)}, u32[]{:S(2)}) %collective-permute-start) | collective-permute-done | bytes 1048608 | tf_op jit(solution)/shard_map/while/body/eval_jaxpr/ppermute | solution.py:14
  332.6 1.1 bitcast_dynamic-update-slice_fusion.2
  334.1 18.8 %collective-permute-start.1 = (bf16[128,2048]{1,0:T(8,128)(2,1)S(1)}, bf16[128,2048]{1,0:T(8,128)(2,1)S(1)}, u32[]{:S(2)}, u32[]{:S(2)}) collective-permute-start(bf16[128,2048]{1,0:T(8,128)(2,1)S(1)} %fusion.47), channel_id=1, source_target_pairs={{0,8},{4,12},{8,16},{12,20},{16,24},{20,28},{1,9},{5,13},{9,17},{1... | collective-permute-start | bytes 1572872 | tf_op jit(solution)/shard_map/while/body/eval_jaxpr/ppermute | solution.py:20
  352.9 6.7 %collective-permute-done.1 = bf16[128,2048]{1,0:T(8,128)(2,1)S(1)} collective-permute-done((bf16[128,2048]{1,0:T(8,128)(2,1)S(1)}, bf16[128,2048]{1,0:T(8,128)(2,1)S(1)}, u32[]{:S(2)}, u32[]{:S(2)}) %collective-permute-start.1) | collective-permute-done | bytes 524320 | tf_op jit(solution)/shard_map/while/body/eval_jaxpr/ppermute | solution.py:20
  362.5 13.4 %collective-permute-done = f32[128,2048]{1,0:T(8,128)S(1)} collective-permute-done((f32[128,2048]{1,0:T(8,128)S(1)}, f32[128,2048]{1,0:T(8,128)S(1)}, u32[]{:S(2)}, u32[]{:S(2)}) %collective-permute-start) | collective-permute-done | bytes 1048608 | tf_op jit(solution)/shard_map/while/body/eval_jaxpr/ppermute | solution.py:14
  376.0 1.1 bitcast_dynamic-update-slice_fusion.2
  377.5 4.4 %collective-permute-start.1 = (bf16[128,2048]{1,0:T(8,128)(2,1)S(1)}, bf16[128,2048]{1,0:T(8,128)(2,1)S(1)}, u32[]{:S(2)}, u32[]{:S(2)}) collective-permute-start(bf16[128,2048]{1,0:T(8,128)(2,1)S(1)} %fusion.47), channel_id=1, source_target_pairs={{0,8},{4,12},{8,16},{12,20},{16,24},{20,28},{1,9},{5,13},{9,17},{1... | collective-permute-start | bytes 1572872 | tf_op jit(solution)/shard_map/while/body/eval_jaxpr/ppermute | solution.py:20
  381.9 6.7 %collective-permute-done.1 = bf16[128,2048]{1,0:T(8,128)(2,1)S(1)} collective-permute-done((bf16[128,2048]{1,0:T(8,128)(2,1)S(1)}, bf16[128,2048]{1,0:T(8,128)(2,1)S(1)}, u32[]{:S(2)}, u32[]{:S(2)}) %collective-permute-start.1) | collective-permute-done | bytes 524320 | tf_op jit(solution)/shard_map/while/body/eval_jaxpr/ppermute | solution.py:20
  388.6 1.2 constant_dynamic-slice_fusion.2
  390.5 1.3 collective-permute-start.3
  391.8 2.1 collective-permute-start.4
  393.9 22.6 %collective-permute-done.3 = bf16[4,128,256]{2,1,0:T(8,128)(2,1)S(1)} collective-permute-done((bf16[4,128,256]{2,1,0:T(8,128)(2,1)S(1)}, bf16[4,128,256]{2,1,0:T(8,128)(2,1)S(1)}, u32[]{:S(2)}, u32[]{:S(2)}) %collective-permute-start.3) | collective-permute-done | bytes 262176 | tf_op jit(solution)/shard_map/ppermute | solution.py:20
  416.5 4.3 %collective-permute-done.4 = bf16[4,128,256]{2,1,0:T(8,128)(2,1)S(1)} collective-permute-done((bf16[4,128,256]{2,1,0:T(8,128)(2,1)S(1)}, bf16[4,128,256]{2,1,0:T(8,128)(2,1)S(1)}, u32[]{:S(2)}, u32[]{:S(2)}) %collective-permute-start.4) | collective-permute-done | bytes 262176 | tf_op jit(solution)/shard_map/ppermute | solution.py:20
  420.8 1.8 select_select_fusion.1
  (140 shorter events, 31.6 us)
Async XLA Ops:
  0.0 8.9 %copy-start = (f32[4,2048]{1,0:T(4,128)S(1)}, f32[4,2048]{1,0:T(4,128)}, u32[]{:S(2)}) copy-start(f32[4,2048]{1,0:T(4,128)} %param.18) | copy-start | bytes 98308
  2.7 52.0 %all-to-all-start = ((bf16[4,128,8,256]{3,1,0,2:T(8,128)(2,1)}), bf16[4,128,8,256]{3,1,0,2:T(8,128)(2,1)S(1)}, u32[]{:S(2)}, u32[]{:S(2)}) async-start(bf16[4,128,8,256]{3,1,0,2:T(8,128)(2,1)} %select_select_fusion), calls=%async_computation | async-start | bytes 4194304 | tf_op jit(solution)/shard_map/all_to_all | solution.py:72
  57.1 1.6 copy-start.1
  57.1 1.6 copy-start.2
  57.1 1.6 copy-start.3
  60.3 25.1 %collective-permute-start = (f32[128,2048]{1,0:T(8,128)S(1)}, f32[128,2048]{1,0:T(8,128)S(1)}, u32[]{:S(2)}, u32[]{:S(2)}) collective-permute-start(f32[128,2048]{1,0:T(8,128)S(1)} %get-tuple-element.623), channel_id=1, source_target_pairs={{0,4},{4,0},{8,12},{12,8},{16,20},{20,16},{24,28},{28,24},{1,5},{5... | collective-permute-start | bytes 3145736 | tf_op jit(solution)/shard_map/while/body/eval_jaxpr/ppermute | solution.py:14
  87.0 27.7 %collective-permute-start.1 = (bf16[128,2048]{1,0:T(8,128)(2,1)S(1)}, bf16[128,2048]{1,0:T(8,128)(2,1)S(1)}, u32[]{:S(2)}, u32[]{:S(2)}) collective-permute-start(bf16[128,2048]{1,0:T(8,128)(2,1)S(1)} %fusion.47), channel_id=1, source_target_pairs={{0,8},{4,12},{8,16},{12,20},{16,24},{20,28},{1,9},{5,13},{9,17},{1... | collective-permute-start | bytes 1572872 | tf_op jit(solution)/shard_map/while/body/eval_jaxpr/ppermute | solution.py:20
  131.4 23.1 %collective-permute-start = (f32[128,2048]{1,0:T(8,128)S(1)}, f32[128,2048]{1,0:T(8,128)S(1)}, u32[]{:S(2)}, u32[]{:S(2)}) collective-permute-start(f32[128,2048]{1,0:T(8,128)S(1)} %get-tuple-element.623), channel_id=1, source_target_pairs={{0,4},{4,0},{8,12},{12,8},{16,20},{20,16},{24,28},{28,24},{1,5},{5... | collective-permute-start | bytes 3145736 | tf_op jit(solution)/shard_map/while/body/eval_jaxpr/ppermute | solution.py:14
  156.0 12.8 %collective-permute-start.1 = (bf16[128,2048]{1,0:T(8,128)(2,1)S(1)}, bf16[128,2048]{1,0:T(8,128)(2,1)S(1)}, u32[]{:S(2)}, u32[]{:S(2)}) collective-permute-start(bf16[128,2048]{1,0:T(8,128)(2,1)S(1)} %fusion.47), channel_id=1, source_target_pairs={{0,8},{4,12},{8,16},{12,20},{16,24},{20,28},{1,9},{5,13},{9,17},{1... | collective-permute-start | bytes 1572872 | tf_op jit(solution)/shard_map/while/body/eval_jaxpr/ppermute | solution.py:20
  185.5 21.4 %collective-permute-start = (f32[128,2048]{1,0:T(8,128)S(1)}, f32[128,2048]{1,0:T(8,128)S(1)}, u32[]{:S(2)}, u32[]{:S(2)}) collective-permute-start(f32[128,2048]{1,0:T(8,128)S(1)} %get-tuple-element.623), channel_id=1, source_target_pairs={{0,4},{4,0},{8,12},{12,8},{16,20},{20,16},{24,28},{28,24},{1,5},{5... | collective-permute-start | bytes 3145736 | tf_op jit(solution)/shard_map/while/body/eval_jaxpr/ppermute | solution.py:14
  208.4 11.1 %collective-permute-start.1 = (bf16[128,2048]{1,0:T(8,128)(2,1)S(1)}, bf16[128,2048]{1,0:T(8,128)(2,1)S(1)}, u32[]{:S(2)}, u32[]{:S(2)}) collective-permute-start(bf16[128,2048]{1,0:T(8,128)(2,1)S(1)} %fusion.47), channel_id=1, source_target_pairs={{0,8},{4,12},{8,16},{12,20},{16,24},{20,28},{1,9},{5,13},{9,17},{1... | collective-permute-start | bytes 1572872 | tf_op jit(solution)/shard_map/while/body/eval_jaxpr/ppermute | solution.py:20
  236.2 19.6 %collective-permute-start = (f32[128,2048]{1,0:T(8,128)S(1)}, f32[128,2048]{1,0:T(8,128)S(1)}, u32[]{:S(2)}, u32[]{:S(2)}) collective-permute-start(f32[128,2048]{1,0:T(8,128)S(1)} %get-tuple-element.623), channel_id=1, source_target_pairs={{0,4},{4,0},{8,12},{12,8},{16,20},{20,16},{24,28},{28,24},{1,5},{5... | collective-permute-start | bytes 3145736 | tf_op jit(solution)/shard_map/while/body/eval_jaxpr/ppermute | solution.py:14
  257.4 11.1 %collective-permute-start.1 = (bf16[128,2048]{1,0:T(8,128)(2,1)S(1)}, bf16[128,2048]{1,0:T(8,128)(2,1)S(1)}, u32[]{:S(2)}, u32[]{:S(2)}) collective-permute-start(bf16[128,2048]{1,0:T(8,128)(2,1)S(1)} %fusion.47), channel_id=1, source_target_pairs={{0,8},{4,12},{8,16},{12,20},{16,24},{20,28},{1,9},{5,13},{9,17},{1... | collective-permute-start | bytes 1572872 | tf_op jit(solution)/shard_map/while/body/eval_jaxpr/ppermute | solution.py:20
  285.1 17.6 %collective-permute-start = (f32[128,2048]{1,0:T(8,128)S(1)}, f32[128,2048]{1,0:T(8,128)S(1)}, u32[]{:S(2)}, u32[]{:S(2)}) collective-permute-start(f32[128,2048]{1,0:T(8,128)S(1)} %get-tuple-element.623), channel_id=1, source_target_pairs={{0,4},{4,0},{8,12},{12,8},{16,20},{20,16},{24,28},{28,24},{1,5},{5... | collective-permute-start | bytes 3145736 | tf_op jit(solution)/shard_map/while/body/eval_jaxpr/ppermute | solution.py:14
  304.3 11.1 %collective-permute-start.1 = (bf16[128,2048]{1,0:T(8,128)(2,1)S(1)}, bf16[128,2048]{1,0:T(8,128)(2,1)S(1)}, u32[]{:S(2)}, u32[]{:S(2)}) collective-permute-start(bf16[128,2048]{1,0:T(8,128)(2,1)S(1)} %fusion.47), channel_id=1, source_target_pairs={{0,8},{4,12},{8,16},{12,20},{16,24},{20,28},{1,9},{5,13},{9,17},{1... | collective-permute-start | bytes 1572872 | tf_op jit(solution)/shard_map/while/body/eval_jaxpr/ppermute | solution.py:20
  316.9 15.6 %collective-permute-start = (f32[128,2048]{1,0:T(8,128)S(1)}, f32[128,2048]{1,0:T(8,128)S(1)}, u32[]{:S(2)}, u32[]{:S(2)}) collective-permute-start(f32[128,2048]{1,0:T(8,128)S(1)} %get-tuple-element.623), channel_id=1, source_target_pairs={{0,4},{4,0},{8,12},{12,8},{16,20},{20,16},{24,28},{28,24},{1,5},{5... | collective-permute-start | bytes 3145736 | tf_op jit(solution)/shard_map/while/body/eval_jaxpr/ppermute | solution.py:14
  334.1 25.5 %collective-permute-start.1 = (bf16[128,2048]{1,0:T(8,128)(2,1)S(1)}, bf16[128,2048]{1,0:T(8,128)(2,1)S(1)}, u32[]{:S(2)}, u32[]{:S(2)}) collective-permute-start(bf16[128,2048]{1,0:T(8,128)(2,1)S(1)} %fusion.47), channel_id=1, source_target_pairs={{0,8},{4,12},{8,16},{12,20},{16,24},{20,28},{1,9},{5,13},{9,17},{1... | collective-permute-start | bytes 1572872 | tf_op jit(solution)/shard_map/while/body/eval_jaxpr/ppermute | solution.py:20
  361.1 14.9 %collective-permute-start = (f32[128,2048]{1,0:T(8,128)S(1)}, f32[128,2048]{1,0:T(8,128)S(1)}, u32[]{:S(2)}, u32[]{:S(2)}) collective-permute-start(f32[128,2048]{1,0:T(8,128)S(1)} %get-tuple-element.623), channel_id=1, source_target_pairs={{0,4},{4,0},{8,12},{12,8},{16,20},{20,16},{24,28},{28,24},{1,5},{5... | collective-permute-start | bytes 3145736 | tf_op jit(solution)/shard_map/while/body/eval_jaxpr/ppermute | solution.py:14
  377.5 11.1 %collective-permute-start.1 = (bf16[128,2048]{1,0:T(8,128)(2,1)S(1)}, bf16[128,2048]{1,0:T(8,128)(2,1)S(1)}, u32[]{:S(2)}, u32[]{:S(2)}) collective-permute-start(bf16[128,2048]{1,0:T(8,128)(2,1)S(1)} %fusion.47), channel_id=1, source_target_pairs={{0,8},{4,12},{8,16},{12,20},{16,24},{20,28},{1,9},{5,13},{9,17},{1... | collective-permute-start | bytes 1572872 | tf_op jit(solution)/shard_map/while/body/eval_jaxpr/ppermute | solution.py:20
  389.8 4.1 collective-permute-start.2
  390.5 26.0 %collective-permute-start.3 = (bf16[4,128,256]{2,1,0:T(8,128)(2,1)S(1)}, bf16[4,128,256]{2,1,0:T(8,128)(2,1)S(1)}, u32[]{:S(2)}, u32[]{:S(2)}) collective-permute-start(bf16[4,128,256]{2,1,0:T(8,128)(2,1)S(1)} %get-tuple-element.476), channel_id=1, source_target_pairs={{16,0},{20,4},{24,8},{28,12},{17,1},{21,5},{25,9},{29,13},{18,2},{... | collective-permute-start | bytes 786440 | tf_op jit(solution)/shard_map/ppermute | solution.py:20
  391.8 29.0 %collective-permute-start.4 = (bf16[4,128,256]{2,1,0:T(8,128)(2,1)S(1)}, bf16[4,128,256]{2,1,0:T(8,128)(2,1)S(1)}, u32[]{:S(2)}, u32[]{:S(2)}) collective-permute-start(bf16[4,128,256]{2,1,0:T(8,128)(2,1)S(1)} %get-tuple-element.475), channel_id=1, source_target_pairs={{8,0},{12,4},{16,8},{20,12},{24,16},{28,20},{9,1},{13,5},{17,9},{2... | collective-permute-start | bytes 786440 | tf_op jit(solution)/shard_map/ppermute | solution.py:20
where the time goes:
time: 424 us; the launch traced here: 423 us
  waiting for transfers between devices  270 us (64%)
  starting transfers between devices  53.2 us (13%)
  matrix products  47.3 us (11%)
  local copies, waits for them, and re-layouts  29.2 us (7%)
  other arithmetic  16.9 us (4%)
  loops' own time  6.02 us (1%)
    ppermute x7, waiting for transfers between devices, partner(): return lax.ppermute(value, axis, pairs)  123 us
    ppermute x10, waiting for transfers between devices, shifted(): return lax.ppermute(value, axis, pairs)  101 us
    all_to_all x1, waiting for transfers between devices, on_device(): lax.all_to_all(outgoing, 'segment', split_axis=2, concat_axis=2, tiled=True)  45.8 us
    ppermute x10, starting transfers between devices, shifted(): return lax.ppermute(value, axis, pairs)  40 us
    dynamic_slice x30, local copies, waits for them, and re-layouts, pick_row(): return lax.dynamic_index_in_dim(array, row_slot, 0, keepdims=False)  21.5 us
    dot_general x4, matrix products, head_partial(): jnp.dot(source, in_weight[:, head_cols:], preferred_element_type=jnp.floa...  18.8 us
    dot_general x4, matrix products, head_partial(): jnp.dot(normed, in_weight[:, :head_cols], preferred_element_type=jnp.floa...  11.8 us
    dot_general x4, matrix products, head_partial(): return jnp.dot(mixture, out_weight, preferred_element_type=jnp.float32)  11.7 us
  transfers between devices with their start and end apart: 18, of which 17 were waited for; matrix products, arithmetic and copies ran while one was open for 2% of the time, Pallas kernels for 0%

commit v1 on v0

--- a/solution.py
+++ b/solution.py
@@ -6,6 +6,17 @@
 HEAD = 64
 epsilon = 1e-06
 score_scale = 0.125
+
+
+def split_up(array, dim, size):
+    before, after = (array.shape[:dim], array.shape[dim + 1 :])
+    return jnp.moveaxis(array.reshape(*before, size, -1, *after), dim, 0)
+
+
+def laid_out(tiles, dim):
+    tiles = jnp.moveaxis(tiles, 0, dim)
+    shape = tiles.shape
+    return tiles.reshape(*shape[:dim], shape[dim] * shape[dim + 1], *shape[dim + 2 :])
 
 
 def partner(value, axis, distance):
@@ -69,7 +80,14 @@
         src_embed[:, :, None, :],
         jnp.where(destination == 2, tgt_embed[:, :, None, :], jnp.zeros((), jnp.bfloat16)),
     )
-    arrived = lax.all_to_all(outgoing, "segment", split_axis=2, concat_axis=2, tiled=True)
+    size, index = (lax.axis_size("segment"), lax.axis_index("segment"))
+    blocks = split_up(outgoing, 2, size)
+    outs = [blocks[index]]
+    for step in range(1, size):
+        sent = blocks[index ^ step]
+        outs.append(lax.ppermute(sent, "segment", [(i_2, i_2 ^ step) for i_2 in range(size)]))
+    blocks = jnp.stack(outs)[index ^ jnp.arange(size)]
+    arrived = laid_out(blocks, 2)
     embedded = arrived.reshape(batches, seq_len, full_width)
     in_weight = attn_in[0]
     out_weight = attn_out[0]

time: 424 us -> 401 us (0.946)
  waiting for transfers between devices: 270 us -> 235 us
  local copies, waits for them, and re-layouts: 29.2 us -> 38.5 us
    all_to_all x1 -> x0, waiting for transfers between devices: 45.8 us -> none  [on_device(): lax.all_to_all(outgoing, 'segment', split_axis=2, concat_axis=2, tiled=True)]
    ppermute x0 -> x7, waiting for transfers between devices: none -> 36.9 us  [on_device(): lax.ppermute(sent, 'segment', [(i_2, i_2 ^ step) for i_2 in range(size)])]
    ppermute x10, waiting for transfers between devices: 101 us -> 82.2 us  [shifted(): return lax.ppermute(value, axis, pairs)]
    ppermute x0 -> x7, starting transfers between devices: none -> 9.08 us  [on_device(): lax.ppermute(sent, 'segment', [(i_2, i_2 ^ step) for i_2 in range(size)])]
    ppermute x7, waiting for transfers between devices: 123 us -> 116 us  [partner(): return lax.ppermute(value, axis, pairs)]
    all_to_all x1 -> x0, starting transfers between devices: 6.25 us -> none  [on_device(): lax.all_to_all(outgoing, 'segment', split_axis=2, concat_axis=2, tiled=True)]
    unnamed x8 -> x15, local copies, waits for them, and re-layouts: 0.02 us -> 5.04 us
  transfers between devices with their start and end apart: 18 -> 24, of which waited for: 17 -> 22; matrix products, arithmetic and copies ran while one was open for 2% -> 3% of each run, Pallas kernels for 0% -> 0%
where the time goes in v1:
time: 401 us; the launch traced here: 398 us
  waiting for transfers between devices  235 us (59%)
  starting transfers between devices  55 us (14%)
  matrix products  47.3 us (12%)
  local copies, waits for them, and re-layouts  38.5 us (10%)
  other arithmetic  15.6 us (4%)
  loops' own time  6.15 us (2%)
    ppermute x7, waiting for transfers between devices, partner(): return lax.ppermute(value, axis, pairs)  116 us
    ppermute x10, waiting for transfers between devices, shifted(): return lax.ppermute(value, axis, pairs)  82.2 us
    ppermute x10, starting transfers between devices, shifted(): return lax.ppermute(value, axis, pairs)  41.4 us
    ppermute x7, waiting for transfers between devices, on_device(): lax.ppermute(sent, 'segment', [(i_2, i_2 ^ step) for i_2 in range(size)])  36.9 us
    dynamic_slice x30, local copies, waits for them, and re-layouts, pick_row(): return lax.dynamic_index_in_dim(array, row_slot, 0, keepdims=False)  21.6 us
    dot_general x4, matrix products, head_partial(): jnp.dot(source, in_weight[:, head_cols:], preferred_element_type=jnp.floa...  18.8 us
    dot_general x4, matrix products, head_partial(): jnp.dot(normed, in_weight[:, :head_cols], preferred_element_type=jnp.floa...  11.8 us
    dot_general x4, matrix products, head_partial(): return jnp.dot(mixture, out_weight, preferred_element_type=jnp.float32)  11.7 us
  transfers between devices with their start and end apart: 24, of which 22 were waited for; matrix products, arithmetic and copies ran while one was open for 3% of the time, Pallas kernels for 0%

profile of v1, /device:TPU:12, one launch (start us, length us, event | category | flops | bytes accessed | tf_op | source)
XLA Modules:
  0.0 398.0 jit_solution(405029556286311442)
XLA Ops:
  0.1 1.3 select_select_fusion
  1.4 1.2 dynamic-slice_bitcast_fusion
  2.5 1.5 collective-permute-start.2
  4.5 1.5 collective-permute-start.4
  6.0 2.6 collective-permute-start.5
  9.4 1.3 collective-permute-start.6
  11.8 1.6 collective-permute-start.7
  13.3 8.4 %collective-permute-done.3 = bf16[4,128,1,256]{3,1,0,2:T(8,128)(2,1)S(1)} collective-permute-done((bf16[4,128,1,256]{3,1,0,2:T(8,128)(2,1)}, bf16[4,128,1,256]{3,1,0,2:T(8,128)(2,1)S(1)}, u32[]{:S(2)}, u32[]{:S(2)}) %collective-permute-start.3) | collective-permute-done | bytes 262176 | tf_op jit(solution)/shard_map/ppermute | solution.py:88
  22.7 3.3 collective-permute-done.4
  27.4 16.3 %collective-permute-done.6 = bf16[4,128,1,256]{3,1,0,2:T(8,128)(2,1)S(1)} collective-permute-done((bf16[4,128,1,256]{3,1,0,2:T(8,128)(2,1)}, bf16[4,128,1,256]{3,1,0,2:T(8,128)(2,1)S(1)}, u32[]{:S(2)}, u32[]{:S(2)}) %collective-permute-start.6) | collective-permute-done | bytes 262176 | tf_op jit(solution)/shard_map/ppermute | solution.py:88
  44.4 4.9 %collective-permute-done.7 = bf16[4,128,1,256]{3,1,0,2:T(8,128)(2,1)S(1)} collective-permute-done((bf16[4,128,1,256]{3,1,0,2:T(8,128)(2,1)}, bf16[4,128,1,256]{3,1,0,2:T(8,128)(2,1)S(1)}, u32[]{:S(2)}, u32[]{:S(2)}) %collective-permute-start.7) | collective-permute-done | bytes 262176 | tf_op jit(solution)/shard_map/ppermute | solution.py:88
  50.1 3.6 collective-permute-done.8
  54.4 2.3 gather_fusion
  56.6 2.4 copy.23
  59.0 1.6 broadcast_in_dim.86
  60.7 304.5 %while.18 = (s32[]{:T(128)}, bf16[128,2048]{1,0:T(8,128)(2,1)S(1)}, bf16[4,128,2048]{2,1,0:T(8,128)(2,1)}, pred[]{:T(512)}, pred[]{:T(512)}, /*index=5*/s32[]{:T...) while((s32[]{:T(128)}, bf16[128,2048]{1,0:T(8,128)(2,1)S(1)}, ...), condition=%wide.region_7.8_spmd.clone, body=%wide.region_0.7_spmd.clone.sunk | while | flops 2257898240 | bytes 44399368 | solution.py:158
  64.2 21.4 %collective-permute-done = f32[128,2048]{1,0:T(8,128)S(1)} collective-permute-done((f32[128,2048]{1,0:T(8,128)S(1)}, f32[128,2048]{1,0:T(8,128)S(1)}, u32[]{:S(2)}, u32[]{:S(2)}) %collective-permute-start) | collective-permute-done | bytes 1048608 | tf_op jit(solution)/shard_map/while/body/eval_jaxpr/ppermute | solution.py:25
  85.6 1.1 bitcast_dynamic-update-slice_fusion.10
  87.1 4.6 %collective-permute-start.1 = (bf16[128,2048]{1,0:T(8,128)(2,1)S(1)}, bf16[128,2048]{1,0:T(8,128)(2,1)S(1)}, u32[]{:S(2)}, u32[]{:S(2)}) collective-permute-start(bf16[128,2048]{1,0:T(8,128)(2,1)S(1)} %fusion.48), channel_id=1, source_target_pairs={{0,8},{4,12},{8,16},{12,20},{16,24},{20,28},{1,9},{5,13},{9,17},{1... | collective-permute-start | bytes 1572872 | tf_op jit(solution)/shard_map/while/body/eval_jaxpr/ppermute | solution.py:31
  91.8 8.7 %collective-permute-done.1 = bf16[128,2048]{1,0:T(8,128)(2,1)S(1)} collective-permute-done((bf16[128,2048]{1,0:T(8,128)(2,1)S(1)}, bf16[128,2048]{1,0:T(8,128)(2,1)S(1)}, u32[]{:S(2)}, u32[]{:S(2)}) %collective-permute-start.1) | collective-permute-done | bytes 524320 | tf_op jit(solution)/shard_map/while/body/eval_jaxpr/ppermute | solution.py:31
  101.8 15.3 %conditional.3 = (f32[128,2048]{1,0:T(8,128)S(1)}) conditional(s32[]{:T(128)} %convert_element_type.120, () %tuple.62, (s32[]{:T(128)}, bf16[128,2048]{1,0:T(8,128)(2,1)S(1)}, f32[2048]{0:T(1024)S(1)}, bf16[128,2048]{1,0:T(8,128)(2,1)S(1)}, bf16[2048,3072]{1,0:T(8,128)(2,1)}, /*index=5*/s32[]{:T(128)}, s32[4]{0:T(128)S(1)}, s32[4]{0:T(128)S(1)}, ...), branch_computations={%region_1.1_spmd, %region_2.5_spmd} | conditional | flops 2254227968 | bytes 27479392 | solution.py:137
  104.7 4.7 %fusion.9 = bf16[128,2048]{1,0:T(8,128)(2,1)S(1)} fusion(bf16[2048,3072]{1,0:T(8,128)(2,1)} %get-tuple-element.369, bf16[128,2048]{1,0:T(8,128)(2,1)S(1)} %get-tuple-element.366, pred[]{:T(512)S(6)} %eq.42, bf16[128,2048]{1,0:T(8,128)(2,1)S(1)} %get-tuple-element.367, f32[2048]{0:T(1024)S(1)} %get-tuple-element.368, f32[128]{0:T(128)S(1)} %add_rsqrt_fusion), kind=kOutput, calls=%fused_computation.8 | convolution fusion | flops 1075314688 | bytes 9970177 | tf_op jit(solution)/shard_map/while/body/eval_jaxpr/cond/branch_1_fun/dot_general | solution.py:113
  109.6 2.9 fusion.15
  114.2 2.9 fusion.36
  117.1 1.4 collective-permute-start
  119.6 19.2 %collective-permute-done = f32[128,2048]{1,0:T(8,128)S(1)} collective-permute-done((f32[128,2048]{1,0:T(8,128)S(1)}, f32[128,2048]{1,0:T(8,128)S(1)}, u32[]{:S(2)}, u32[]{:S(2)}) %collective-permute-start) | collective-permute-done | bytes 1048608 | tf_op jit(solution)/shard_map/while/body/eval_jaxpr/ppermute | solution.py:25
  138.7 1.1 bitcast_dynamic-update-slice_fusion.10
  140.3 1.9 collective-permute-start.1
  142.2 9.4 %collective-permute-done.1 = bf16[128,2048]{1,0:T(8,128)(2,1)S(1)} collective-permute-done((bf16[128,2048]{1,0:T(8,128)(2,1)S(1)}, bf16[128,2048]{1,0:T(8,128)(2,1)S(1)}, u32[]{:S(2)}, u32[]{:S(2)}) %collective-permute-start.1) | collective-permute-done | bytes 524320 | tf_op jit(solution)/shard_map/while/body/eval_jaxpr/ppermute | solution.py:31
  153.1 15.3 %conditional.3 = (f32[128,2048]{1,0:T(8,128)S(1)}) conditional(s32[]{:T(128)} %convert_element_type.120, () %tuple.62, (s32[]{:T(128)}, bf16[128,2048]{1,0:T(8,128)(2,1)S(1)}, f32[2048]{0:T(1024)S(1)}, bf16[128,2048]{1,0:T(8,128)(2,1)S(1)}, bf16[2048,3072]{1,0:T(8,128)(2,1)}, /*index=5*/s32[]{:T(128)}, s32[4]{0:T(128)S(1)}, s32[4]{0:T(128)S(1)}, ...), branch_computations={%region_1.1_spmd, %region_2.5_spmd} | conditional | flops 2254227968 | bytes 27479392 | solution.py:137
  155.9 4.7 %fusion.9 = bf16[128,2048]{1,0:T(8,128)(2,1)S(1)} fusion(bf16[2048,3072]{1,0:T(8,128)(2,1)} %get-tuple-element.369, bf16[128,2048]{1,0:T(8,128)(2,1)S(1)} %get-tuple-element.366, pred[]{:T(512)S(6)} %eq.42, bf16[128,2048]{1,0:T(8,128)(2,1)S(1)} %get-tuple-element.367, f32[2048]{0:T(1024)S(1)} %get-tuple-element.368, f32[128]{0:T(128)S(1)} %add_rsqrt_fusion), kind=kOutput, calls=%fused_computation.8 | convolution fusion | flops 1075314688 | bytes 9970177 | tf_op jit(solution)/shard_map/while/body/eval_jaxpr/cond/branch_1_fun/dot_general | solution.py:113
  160.8 3.0 fusion.15
  165.4 2.9 fusion.36
  169.7 18.5 %collective-permute-done = f32[128,2048]{1,0:T(8,128)S(1)} collective-permute-done((f32[128,2048]{1,0:T(8,128)S(1)}, f32[128,2048]{1,0:T(8,128)S(1)}, u32[]{:S(2)}, u32[]{:S(2)}) %collective-permute-start) | collective-permute-done | bytes 1048608 | tf_op jit(solution)/shard_map/while/body/eval_jaxpr/ppermute | solution.py:25
  188.2 1.1 bitcast_dynamic-update-slice_fusion.10
  189.8 2.5 collective-permute-start.1
  192.3 8.6 %collective-permute-done.1 = bf16[128,2048]{1,0:T(8,128)(2,1)S(1)} collective-permute-done((bf16[128,2048]{1,0:T(8,128)(2,1)S(1)}, bf16[128,2048]{1,0:T(8,128)(2,1)S(1)}, u32[]{:S(2)}, u32[]{:S(2)}) %collective-permute-start.1) | collective-permute-done | bytes 524320 | tf_op jit(solution)/shard_map/while/body/eval_jaxpr/ppermute | solution.py:31
  202.3 15.3 %conditional.3 = (f32[128,2048]{1,0:T(8,128)S(1)}) conditional(s32[]{:T(128)} %convert_element_type.120, () %tuple.62, (s32[]{:T(128)}, bf16[128,2048]{1,0:T(8,128)(2,1)S(1)}, f32[2048]{0:T(1024)S(1)}, bf16[128,2048]{1,0:T(8,128)(2,1)S(1)}, bf16[2048,3072]{1,0:T(8,128)(2,1)}, /*index=5*/s32[]{:T(128)}, s32[4]{0:T(128)S(1)}, s32[4]{0:T(128)S(1)}, ...), branch_computations={%region_1.1_spmd, %region_2.5_spmd} | conditional | flops 2254227968 | bytes 27479392 | solution.py:137
  205.1 4.7 %fusion.9 = bf16[128,2048]{1,0:T(8,128)(2,1)S(1)} fusion(bf16[2048,3072]{1,0:T(8,128)(2,1)} %get-tuple-element.369, bf16[128,2048]{1,0:T(8,128)(2,1)S(1)} %get-tuple-element.366, pred[]{:T(512)S(6)} %eq.42, bf16[128,2048]{1,0:T(8,128)(2,1)S(1)} %get-tuple-element.367, f32[2048]{0:T(1024)S(1)} %get-tuple-element.368, f32[128]{0:T(128)S(1)} %add_rsqrt_fusion), kind=kOutput, calls=%fused_computation.8 | convolution fusion | flops 1075314688 | bytes 9970177 | tf_op jit(solution)/shard_map/while/body/eval_jaxpr/cond/branch_1_fun/dot_general | solution.py:113
  210.1 2.9 fusion.15
  214.6 2.9 fusion.36
  219.0 16.5 %collective-permute-done = f32[128,2048]{1,0:T(8,128)S(1)} collective-permute-done((f32[128,2048]{1,0:T(8,128)S(1)}, f32[128,2048]{1,0:T(8,128)S(1)}, u32[]{:S(2)}, u32[]{:S(2)}) %collective-permute-start) | collective-permute-done | bytes 1048608 | tf_op jit(solution)/shard_map/while/body/eval_jaxpr/ppermute | solution.py:25
  235.5 1.1 bitcast_dynamic-update-slice_fusion.10
  237.0 2.8 collective-permute-start.1
  239.8 8.3 %collective-permute-done.1 = bf16[128,2048]{1,0:T(8,128)(2,1)S(1)} collective-permute-done((bf16[128,2048]{1,0:T(8,128)(2,1)S(1)}, bf16[128,2048]{1,0:T(8,128)(2,1)S(1)}, u32[]{:S(2)}, u32[]{:S(2)}) %collective-permute-start.1) | collective-permute-done | bytes 524320 | tf_op jit(solution)/shard_map/while/body/eval_jaxpr/ppermute | solution.py:31
  249.5 15.3 %conditional.3 = (f32[128,2048]{1,0:T(8,128)S(1)}) conditional(s32[]{:T(128)} %convert_element_type.120, () %tuple.62, (s32[]{:T(128)}, bf16[128,2048]{1,0:T(8,128)(2,1)S(1)}, f32[2048]{0:T(1024)S(1)}, bf16[128,2048]{1,0:T(8,128)(2,1)S(1)}, bf16[2048,3072]{1,0:T(8,128)(2,1)}, /*index=5*/s32[]{:T(128)}, s32[4]{0:T(128)S(1)}, s32[4]{0:T(128)S(1)}, ...), branch_computations={%region_1.1_spmd, %region_2.5_spmd} | conditional | flops 2254227968 | bytes 27479392 | solution.py:137
  252.4 4.7 %fusion.9 = bf16[128,2048]{1,0:T(8,128)(2,1)S(1)} fusion(bf16[2048,3072]{1,0:T(8,128)(2,1)} %get-tuple-element.369, bf16[128,2048]{1,0:T(8,128)(2,1)S(1)} %get-tuple-element.366, pred[]{:T(512)S(6)} %eq.42, bf16[128,2048]{1,0:T(8,128)(2,1)S(1)} %get-tuple-element.367, f32[2048]{0:T(1024)S(1)} %get-tuple-element.368, f32[128]{0:T(128)S(1)} %add_rsqrt_fusion), kind=kOutput, calls=%fused_computation.8 | convolution fusion | flops 1075314688 | bytes 9970177 | tf_op jit(solution)/shard_map/while/body/eval_jaxpr/cond/branch_1_fun/dot_general | solution.py:113
  257.3 3.0 fusion.15
  261.9 2.9 fusion.36
  266.3 14.4 %collective-permute-done = f32[128,2048]{1,0:T(8,128)S(1)} collective-permute-done((f32[128,2048]{1,0:T(8,128)S(1)}, f32[128,2048]{1,0:T(8,128)S(1)}, u32[]{:S(2)}, u32[]{:S(2)}) %collective-permute-start) | collective-permute-done | bytes 1048608 | tf_op jit(solution)/shard_map/while/body/eval_jaxpr/ppermute | solution.py:25
  282.2 3.1 collective-permute-start.1
  285.3 8.0 %collective-permute-done.1 = bf16[128,2048]{1,0:T(8,128)(2,1)S(1)} collective-permute-done((bf16[128,2048]{1,0:T(8,128)(2,1)S(1)}, bf16[128,2048]{1,0:T(8,128)(2,1)S(1)}, u32[]{:S(2)}, u32[]{:S(2)}) %collective-permute-start.1) | collective-permute-done | bytes 524320 | tf_op jit(solution)/shard_map/while/body/eval_jaxpr/ppermute | solution.py:31
  296.3 13.4 %collective-permute-done = f32[128,2048]{1,0:T(8,128)S(1)} collective-permute-done((f32[128,2048]{1,0:T(8,128)S(1)}, f32[128,2048]{1,0:T(8,128)S(1)}, u32[]{:S(2)}, u32[]{:S(2)}) %collective-permute-start) | collective-permute-done | bytes 1048608 | tf_op jit(solution)/shard_map/while/body/eval_jaxpr/ppermute | solution.py:25
  311.3 18.2 %collective-permute-start.1 = (bf16[128,2048]{1,0:T(8,128)(2,1)S(1)}, bf16[128,2048]{1,0:T(8,128)(2,1)S(1)}, u32[]{:S(2)}, u32[]{:S(2)}) collective-permute-start(bf16[128,2048]{1,0:T(8,128)(2,1)S(1)} %fusion.48), channel_id=1, source_target_pairs={{0,8},{4,12},{8,16},{12,20},{16,24},{20,28},{1,9},{5,13},{9,17},{1... | collective-permute-start | bytes 1572872 | tf_op jit(solution)/shard_map/while/body/eval_jaxpr/ppermute | solution.py:31
  329.5 6.7 %collective-permute-done.1 = bf16[128,2048]{1,0:T(8,128)(2,1)S(1)} collective-permute-done((bf16[128,2048]{1,0:T(8,128)(2,1)S(1)}, bf16[128,2048]{1,0:T(8,128)(2,1)S(1)}, u32[]{:S(2)}, u32[]{:S(2)}) %collective-permute-start.1) | collective-permute-done | bytes 524320 | tf_op jit(solution)/shard_map/while/body/eval_jaxpr/ppermute | solution.py:31
  339.7 12.9 %collective-permute-done = f32[128,2048]{1,0:T(8,128)S(1)} collective-permute-done((f32[128,2048]{1,0:T(8,128)S(1)}, f32[128,2048]{1,0:T(8,128)S(1)}, u32[]{:S(2)}, u32[]{:S(2)}) %collective-permute-start) | collective-permute-done | bytes 1048608 | tf_op jit(solution)/shard_map/while/body/eval_jaxpr/ppermute | solution.py:25
  354.1 4.4 %collective-permute-start.1 = (bf16[128,2048]{1,0:T(8,128)(2,1)S(1)}, bf16[128,2048]{1,0:T(8,128)(2,1)S(1)}, u32[]{:S(2)}, u32[]{:S(2)}) collective-permute-start(bf16[128,2048]{1,0:T(8,128)(2,1)S(1)} %fusion.48), channel_id=1, source_target_pairs={{0,8},{4,12},{8,16},{12,20},{16,24},{20,28},{1,9},{5,13},{9,17},{1... | collective-permute-start | bytes 1572872 | tf_op jit(solution)/shard_map/while/body/eval_jaxpr/ppermute | solution.py:31
  358.5 6.7 %collective-permute-done.1 = bf16[128,2048]{1,0:T(8,128)(2,1)S(1)} collective-permute-done((bf16[128,2048]{1,0:T(8,128)(2,1)S(1)}, bf16[128,2048]{1,0:T(8,128)(2,1)S(1)}, u32[]{:S(2)}, u32[]{:S(2)}) %collective-permute-start.1) | collective-permute-done | bytes 524320 | tf_op jit(solution)/shard_map/while/body/eval_jaxpr/ppermute | solution.py:31
  365.2 1.2 constant_dynamic-slice_fusion.2
  366.4 1.3 collective-permute-start.10
  367.7 1.9 collective-permute-start.11
  370.3 19.5 %collective-permute-done.10 = bf16[4,128,256]{2,1,0:T(8,128)(2,1)S(1)} collective-permute-done((bf16[4,128,256]{2,1,0:T(8,128)(2,1)S(1)}, bf16[4,128,256]{2,1,0:T(8,128)(2,1)S(1)}, u32[]{:S(2)}, u32[]{:S(2)}) %collective-permute-start.10) | collective-permute-done | bytes 262176 | tf_op jit(solution)/shard_map/ppermute | solution.py:31
  389.8 6.4 %collective-permute-done.11 = bf16[4,128,256]{2,1,0:T(8,128)(2,1)S(1)} collective-permute-done((bf16[4,128,256]{2,1,0:T(8,128)(2,1)S(1)}, bf16[4,128,256]{2,1,0:T(8,128)(2,1)S(1)}, u32[]{:S(2)}, u32[]{:S(2)}) %collective-permute-start.11) | collective-permute-done | bytes 262176 | tf_op jit(solution)/shard_map/ppermute | solution.py:31
  396.2 1.8 select_select_fusion.1
  (164 shorter events, 48.3 us)
Async XLA Ops:
  0.0 8.6 %copy-start = (f32[4,2048]{1,0:T(4,128)S(1)}, f32[4,2048]{1,0:T(4,128)}, u32[]{:S(2)}) copy-start(f32[4,2048]{1,0:T(4,128)} %param.18) | copy-start | bytes 98308
  2.5 8.5 %collective-permute-start.2 = (bf16[4,128,1,256]{3,1,0,2:T(8,128)(2,1)}, bf16[4,128,1,256]{3,1,0,2:T(8,128)(2,1)S(1)}, u32[]{:S(2)}, u32[]{:S(2)}) collective-permute-start(bf16[4,128,1,256]{3,1,0,2:T(8,128)(2,1)} %get-tuple-element.484), channel_id=1, source_target_pairs={{0,4},{4,0},{8,12},{12,8},{16,20},{20,16},{24,28},{28,24},{1,5},{5... | collective-permute-start | bytes 786440 | tf_op jit(solution)/shard_map/ppermute | solution.py:88
  4.0 17.7 %collective-permute-start.3 = (bf16[4,128,1,256]{3,1,0,2:T(8,128)(2,1)}, bf16[4,128,1,256]{3,1,0,2:T(8,128)(2,1)S(1)}, u32[]{:S(2)}, u32[]{:S(2)}) collective-permute-start(bf16[4,128,1,256]{3,1,0,2:T(8,128)(2,1)} %get-tuple-element.483), channel_id=1, source_target_pairs={{0,8},{4,12},{8,0},{12,4},{16,24},{20,28},{24,16},{28,20},{1,9},{5... | collective-permute-start | bytes 786440 | tf_op jit(solution)/shard_map/ppermute | solution.py:88
  4.5 21.5 %collective-permute-start.4 = (bf16[4,128,1,256]{3,1,0,2:T(8,128)(2,1)}, bf16[4,128,1,256]{3,1,0,2:T(8,128)(2,1)S(1)}, u32[]{:S(2)}, u32[]{:S(2)}) collective-permute-start(bf16[4,128,1,256]{3,1,0,2:T(8,128)(2,1)} %get-tuple-element.482), channel_id=1, source_target_pairs={{0,12},{4,8},{8,4},{12,0},{16,28},{20,24},{24,20},{28,16},{1,13},{... | collective-permute-start | bytes 786440 | tf_op jit(solution)/shard_map/ppermute | solution.py:88
  6.0 20.7 %collective-permute-start.5 = (bf16[4,128,1,256]{3,1,0,2:T(8,128)(2,1)}, bf16[4,128,1,256]{3,1,0,2:T(8,128)(2,1)S(1)}, u32[]{:S(2)}, u32[]{:S(2)}) collective-permute-start(bf16[4,128,1,256]{3,1,0,2:T(8,128)(2,1)} %get-tuple-element.481), channel_id=1, source_target_pairs={{0,16},{4,20},{8,24},{12,28},{16,0},{20,4},{24,8},{28,12},{1,17},{... | collective-permute-start | bytes 786440 | tf_op jit(solution)/shard_map/ppermute | solution.py:88
  9.4 34.3 %collective-permute-start.6 = (bf16[4,128,1,256]{3,1,0,2:T(8,128)(2,1)}, bf16[4,128,1,256]{3,1,0,2:T(8,128)(2,1)S(1)}, u32[]{:S(2)}, u32[]{:S(2)}) collective-permute-start(bf16[4,128,1,256]{3,1,0,2:T(8,128)(2,1)} %get-tuple-element.480), channel_id=1, source_target_pairs={{0,20},{4,16},{8,28},{12,24},{16,4},{20,0},{24,12},{28,8},{1,21},{... | collective-permute-start | bytes 786440 | tf_op jit(solution)/shard_map/ppermute | solution.py:88
  11.8 37.6 %collective-permute-start.7 = (bf16[4,128,1,256]{3,1,0,2:T(8,128)(2,1)}, bf16[4,128,1,256]{3,1,0,2:T(8,128)(2,1)S(1)}, u32[]{:S(2)}, u32[]{:S(2)}) collective-permute-start(bf16[4,128,1,256]{3,1,0,2:T(8,128)(2,1)} %get-tuple-element.479), channel_id=1, source_target_pairs={{0,24},{4,28},{8,16},{12,20},{16,8},{20,12},{24,0},{28,4},{1,25},{... | collective-permute-start | bytes 786440 | tf_op jit(solution)/shard_map/ppermute | solution.py:88
  22.5 31.1 %collective-permute-start.8 = (bf16[4,128,1,256]{3,1,0,2:T(8,128)(2,1)S(1)}, bf16[4,128,1,256]{3,1,0,2:T(8,128)(2,1)S(1)}, u32[]{:S(2)}, u32[]{:S(2)}) collective-permute-start(bf16[4,128,1,256]{3,1,0,2:T(8,128)(2,1)S(1)} %get-tuple-element.478), channel_id=1, source_target_pairs={{0,28},{4,24},{8,20},{12,16},{16,12},{20,8},{24,4},{28,0},{1,29},{... | collective-permute-start | bytes 786440 | tf_op jit(solution)/shard_map/ppermute | solution.py:88
  59.0 1.6 copy-start.1
  59.0 1.6 copy-start.2
  59.0 1.6 copy-start.3
  62.3 23.3 %collective-permute-start = (f32[128,2048]{1,0:T(8,128)S(1)}, f32[128,2048]{1,0:T(8,128)S(1)}, u32[]{:S(2)}, u32[]{:S(2)}) collective-permute-start(f32[128,2048]{1,0:T(8,128)S(1)} %get-tuple-element.630), channel_id=1, source_target_pairs={{0,4},{4,0},{8,12},{12,8},{16,20},{20,16},{24,28},{28,24},{1,5},{5... | collective-permute-start | bytes 3145736 | tf_op jit(solution)/shard_map/while/body/eval_jaxpr/ppermute | solution.py:25
  87.1 13.3 %collective-permute-start.1 = (bf16[128,2048]{1,0:T(8,128)(2,1)S(1)}, bf16[128,2048]{1,0:T(8,128)(2,1)S(1)}, u32[]{:S(2)}, u32[]{:S(2)}) collective-permute-start(bf16[128,2048]{1,0:T(8,128)(2,1)S(1)} %fusion.48), channel_id=1, source_target_pairs={{0,8},{4,12},{8,16},{12,20},{16,24},{20,28},{1,9},{5,13},{9,17},{1... | collective-permute-start | bytes 1572872 | tf_op jit(solution)/shard_map/while/body/eval_jaxpr/ppermute | solution.py:31
  117.1 21.6 %collective-permute-start = (f32[128,2048]{1,0:T(8,128)S(1)}, f32[128,2048]{1,0:T(8,128)S(1)}, u32[]{:S(2)}, u32[]{:S(2)}) collective-permute-start(f32[128,2048]{1,0:T(8,128)S(1)} %get-tuple-element.630), channel_id=1, source_target_pairs={{0,4},{4,0},{8,12},{12,8},{16,20},{20,16},{24,28},{28,24},{1,5},{5... | collective-permute-start | bytes 3145736 | tf_op jit(solution)/shard_map/while/body/eval_jaxpr/ppermute | solution.py:25
  140.3 11.3 %collective-permute-start.1 = (bf16[128,2048]{1,0:T(8,128)(2,1)S(1)}, bf16[128,2048]{1,0:T(8,128)(2,1)S(1)}, u32[]{:S(2)}, u32[]{:S(2)}) collective-permute-start(bf16[128,2048]{1,0:T(8,128)(2,1)S(1)} %fusion.48), channel_id=1, source_target_pairs={{0,8},{4,12},{8,16},{12,20},{16,24},{20,28},{1,9},{5,13},{9,17},{1... | collective-permute-start | bytes 1572872 | tf_op jit(solution)/shard_map/while/body/eval_jaxpr/ppermute | solution.py:31
  168.3 19.9 %collective-permute-start = (f32[128,2048]{1,0:T(8,128)S(1)}, f32[128,2048]{1,0:T(8,128)S(1)}, u32[]{:S(2)}, u32[]{:S(2)}) collective-permute-start(f32[128,2048]{1,0:T(8,128)S(1)} %get-tuple-element.630), channel_id=1, source_target_pairs={{0,4},{4,0},{8,12},{12,8},{16,20},{20,16},{24,28},{28,24},{1,5},{5... | collective-permute-start | bytes 3145736 | tf_op jit(solution)/shard_map/while/body/eval_jaxpr/ppermute | solution.py:25
  189.8 11.1 %collective-permute-start.1 = (bf16[128,2048]{1,0:T(8,128)(2,1)S(1)}, bf16[128,2048]{1,0:T(8,128)(2,1)S(1)}, u32[]{:S(2)}, u32[]{:S(2)}) collective-permute-start(bf16[128,2048]{1,0:T(8,128)(2,1)S(1)} %fusion.48), channel_id=1, source_target_pairs={{0,8},{4,12},{8,16},{12,20},{16,24},{20,28},{1,9},{5,13},{9,17},{1... | collective-permute-start | bytes 1572872 | tf_op jit(solution)/shard_map/while/body/eval_jaxpr/ppermute | solution.py:31
  217.6 17.9 %collective-permute-start = (f32[128,2048]{1,0:T(8,128)S(1)}, f32[128,2048]{1,0:T(8,128)S(1)}, u32[]{:S(2)}, u32[]{:S(2)}) collective-permute-start(f32[128,2048]{1,0:T(8,128)S(1)} %get-tuple-element.630), channel_id=1, source_target_pairs={{0,4},{4,0},{8,12},{12,8},{16,20},{20,16},{24,28},{28,24},{1,5},{5... | collective-permute-start | bytes 3145736 | tf_op jit(solution)/shard_map/while/body/eval_jaxpr/ppermute | solution.py:25
  237.0 11.1 %collective-permute-start.1 = (bf16[128,2048]{1,0:T(8,128)(2,1)S(1)}, bf16[128,2048]{1,0:T(8,128)(2,1)S(1)}, u32[]{:S(2)}, u32[]{:S(2)}) collective-permute-start(bf16[128,2048]{1,0:T(8,128)(2,1)S(1)} %fusion.48), channel_id=1, source_target_pairs={{0,8},{4,12},{8,16},{12,20},{16,24},{20,28},{1,9},{5,13},{9,17},{1... | collective-permute-start | bytes 1572872 | tf_op jit(solution)/shard_map/while/body/eval_jaxpr/ppermute | solution.py:31
  264.8 15.9 %collective-permute-start = (f32[128,2048]{1,0:T(8,128)S(1)}, f32[128,2048]{1,0:T(8,128)S(1)}, u32[]{:S(2)}, u32[]{:S(2)}) collective-permute-start(f32[128,2048]{1,0:T(8,128)S(1)} %get-tuple-element.630), channel_id=1, source_target_pairs={{0,4},{4,0},{8,12},{12,8},{16,20},{20,16},{24,28},{28,24},{1,5},{5... | collective-permute-start | bytes 3145736 | tf_op jit(solution)/shard_map/while/body/eval_jaxpr/ppermute | solution.py:25
  282.2 11.1 %collective-permute-start.1 = (bf16[128,2048]{1,0:T(8,128)(2,1)S(1)}, bf16[128,2048]{1,0:T(8,128)(2,1)S(1)}, u32[]{:S(2)}, u32[]{:S(2)}) collective-permute-start(bf16[128,2048]{1,0:T(8,128)(2,1)S(1)} %fusion.48), channel_id=1, source_target_pairs={{0,8},{4,12},{8,16},{12,20},{16,24},{20,28},{1,9},{5,13},{9,17},{1... | collective-permute-start | bytes 1572872 | tf_op jit(solution)/shard_map/while/body/eval_jaxpr/ppermute | solution.py:31
  294.9 14.9 %collective-permute-start = (f32[128,2048]{1,0:T(8,128)S(1)}, f32[128,2048]{1,0:T(8,128)S(1)}, u32[]{:S(2)}, u32[]{:S(2)}) collective-permute-start(f32[128,2048]{1,0:T(8,128)S(1)} %get-tuple-element.630), channel_id=1, source_target_pairs={{0,4},{4,0},{8,12},{12,8},{16,20},{20,16},{24,28},{28,24},{1,5},{5... | collective-permute-start | bytes 3145736 | tf_op jit(solution)/shard_map/while/body/eval_jaxpr/ppermute | solution.py:25
  311.3 24.9 %collective-permute-start.1 = (bf16[128,2048]{1,0:T(8,128)(2,1)S(1)}, bf16[128,2048]{1,0:T(8,128)(2,1)S(1)}, u32[]{:S(2)}, u32[]{:S(2)}) collective-permute-start(bf16[128,2048]{1,0:T(8,128)(2,1)S(1)} %fusion.48), channel_id=1, source_target_pairs={{0,8},{4,12},{8,16},{12,20},{16,24},{20,28},{1,9},{5,13},{9,17},{1... | collective-permute-start | bytes 1572872 | tf_op jit(solution)/shard_map/while/body/eval_jaxpr/ppermute | solution.py:31
  337.7 14.9 %collective-permute-start = (f32[128,2048]{1,0:T(8,128)S(1)}, f32[128,2048]{1,0:T(8,128)S(1)}, u32[]{:S(2)}, u32[]{:S(2)}) collective-permute-start(f32[128,2048]{1,0:T(8,128)S(1)} %get-tuple-element.630), channel_id=1, source_target_pairs={{0,4},{4,0},{8,12},{12,8},{16,20},{20,16},{24,28},{28,24},{1,5},{5... | collective-permute-start | bytes 3145736 | tf_op jit(solution)/shard_map/while/body/eval_jaxpr/ppermute | solution.py:25
  354.1 11.1 %collective-permute-start.1 = (bf16[128,2048]{1,0:T(8,128)(2,1)S(1)}, bf16[128,2048]{1,0:T(8,128)(2,1)S(1)}, u32[]{:S(2)}, u32[]{:S(2)}) collective-permute-start(bf16[128,2048]{1,0:T(8,128)(2,1)S(1)} %fusion.48), channel_id=1, source_target_pairs={{0,8},{4,12},{8,16},{12,20},{16,24},{20,28},{1,9},{5,13},{9,17},{1... | collective-permute-start | bytes 1572872 | tf_op jit(solution)/shard_map/while/body/eval_jaxpr/ppermute | solution.py:31
  366.4 23.4 %collective-permute-start.10 = (bf16[4,128,256]{2,1,0:T(8,128)(2,1)S(1)}, bf16[4,128,256]{2,1,0:T(8,128)(2,1)S(1)}, u32[]{:S(2)}, u32[]{:S(2)}) collective-permute-start(bf16[4,128,256]{2,1,0:T(8,128)(2,1)S(1)} %get-tuple-element.476), channel_id=1, source_target_pairs={{16,0},{20,4},{24,8},{28,12},{17,1},{21,5},{25,9},{29,13},{18,2},{... | collective-permute-start | bytes 786440 | tf_op jit(solution)/shard_map/ppermute | solution.py:31
  367.7 28.5 %collective-permute-start.11 = (bf16[4,128,256]{2,1,0:T(8,128)(2,1)S(1)}, bf16[4,128,256]{2,1,0:T(8,128)(2,1)S(1)}, u32[]{:S(2)}, u32[]{:S(2)}) collective-permute-start(bf16[4,128,256]{2,1,0:T(8,128)(2,1)S(1)} %get-tuple-element.475), channel_id=1, source_target_pairs={{8,0},{12,4},{16,8},{20,12},{24,16},{28,20},{9,1},{13,5},{17,9},{2... | collective-permute-start | bytes 786440 | tf_op jit(solution)/shard_map/ppermute | solution.py:31
  369.6 26.6 %collective-permute-start.9 = (bf16[4,128,256]{2,1,0:T(8,128)(2,1)S(1)}, bf16[4,128,256]{2,1,0:T(8,128)(2,1)S(1)}, u32[]{:S(2)}, u32[]{:S(2)}) collective-permute-start(bf16[4,128,256]{2,1,0:T(8,128)(2,1)S(1)} %get-tuple-element.477), channel_id=1, source_target_pairs={{24,0},{28,4},{25,1},{29,5},{26,2},{30,6},{27,3},{31,7}} | collective-permute-start | bytes 786440 | tf_op jit(solution)/shard_map/ppermute | solution.py:31
